TPU v7x, 32 devices: a whole 2x2x4 slice. The times are simulated.
32 devices in a mesh: samp: 8 (over y, x, core), cpg: 4 (over z).
Axes of the slice: x: 2, y: 2, z: 4, core: 2. Of those that a mesh axis runs over, the one named last changes fastest.
Arguments:
- responses: bfloat16 [256, 16384], P('samp', 'cpg'), may hold values from -5 to 5
- weights: bfloat16 [256, 16384], P('samp', 'cpg'), may hold values from 1 to 8
- phenotype: float32 [16384], P('cpg'), may hold values from -6 to 6
- eigvecs: bfloat16 [16384, 16384], P('cpg', 'samp'), may hold values from -0.046875 to 0.046875
- eigvals: float32 [16384], P('samp'), may hold values from 0.0001 to 1
- positions: int32 [256], replicated, may hold values from 1 to 76800, as said below
- reaches: int32 [256], P('cpg'), may hold values from 1 to 8
Outputs:
- smoothed: float32 [256], P('cpg')
- log_scale: float32 [256], P('cpg')
Inputs may be any that keep to these rules, and one draw needn't show every extreme that they name: CpG m (from 0) lies at 300 m plus an offset of 1 to 300, so positions strictly increase and consecutive CpGs lie 1 to 599 base pairs apart.
All inputs are finite; a program needn't handle non-finite values.
Results may differ from a plain program's by a relative error of at most 0.0041.
Values may be sent and summed in bfloat16 or wider, within the bound.
A program may use at most 64 MiB of HBM per device.

v0:
```python
import functools

import jax
import jax.numpy as jnp
from jax import lax
from jax.experimental import pallas as pl
from jax.experimental.pallas import tpu as pltpu
from jax.sharding import PartitionSpec as P

ITERS = 4
HALO = 8
EPSILON = 1e-06
band_width = 1000.0
MESH = pl.DeviceIdType.MESH
LANES = 128


def fit_kernel(n, cpgs, a_ref, b_ref, lam_ref, band_ref, out_ref, p_ref, q_ref, r_ref, l_ref, send, recv, edge, zsend, ssem, rsem, esem, fsem):
    me = lax.axis_index("samp")
    mz = lax.axis_index("cpg")
    block = a_ref.shape[0]
    fold = LANES // block
    rows = a_ref.shape[1] // fold
    edge[...] = jnp.zeros_like(edge)

    barrier = pltpu.get_barrier_semaphore()
    for j in range(1, n):
        pl.semaphore_signal(barrier, inc=1, device_id={"samp": lax.rem(me + j, n)}, device_id_type=MESH)

    for other in (lax.rem(mz + 1, cpgs), lax.rem(mz + cpgs - 1, cpgs)):
        pl.semaphore_signal(barrier, inc=1, device_id={"cpg": other}, device_id_type=MESH)

    def folded(ref):
        parts = [ref[:, pl.ds(g * rows, rows)].astype(jnp.float32) for g in range(fold)]
        return jnp.concatenate(parts, axis=0).T

    a = folded(a_ref)
    b = folded(b_ref)
    p_ref[...] = a * b
    q_ref[...] = b * b
    r_ref[...] = a * a
    lam_parts = [jnp.broadcast_to(lam_ref[:, pl.ds(g * rows, rows)], (block, rows)) for g in range(fold)]
    l_ref[...] = jnp.concatenate(lam_parts, axis=0).T

    pl.semaphore_wait(barrier, n + 1)

    step = 64

    def sums(log_scale, full):
        scale = jnp.exp(log_scale)

        def body(i, acc):
            at = pl.ds(pl.multiple_of(i * step, step), step)
            lam = l_ref[at, :]
            inv = 1.0 / (scale * lam + 1.0)
            p = p_ref[at, :]
            q = q_ref[at, :]
            terms = [p * inv, q * inv]
            if full:
                lev = lam * inv
                s = lev * inv
                terms += [lev, lev * lev, s * r_ref[at, :], s * p, s * q]
            terms = [t.reshape(step // 8, 8, LANES).sum(axis=0) for t in terms]
            return tuple(x + y for x, y in zip(acc, terms))

        count = 7 if full else 2
        acc = lax.fori_loop(0, rows // step, body, tuple(jnp.zeros((8, LANES), jnp.float32) for _ in range(count)))
        flat = []
        for x in acc:
            row = jnp.sum(x, axis=0, keepdims=True)
            total = row
            for g in range(1, fold):
                total = total + pltpu.roll(row, g * block, 1)
            flat.append(total)
        flat += [jnp.zeros((1, LANES), jnp.float32)] * (8 - count)
        return jnp.concatenate(flat, axis=0)

    def total(it, value):
        send[it] = value
        copies = []
        for j in range(1, n):
            copies.append(pltpu.make_async_remote_copy(
                src_ref=send.at[it], dst_ref=recv.at[it, j],
                send_sem=ssem.at[it, j], recv_sem=rsem.at[it, j],
                device_id={"samp": lax.rem(me + j, n)}, device_id_type=MESH))
        for c in copies:
            c.start()
        recv[it, 0] = value
        for c in copies:
            c.wait_recv()
        out = jnp.zeros((8, LANES), jnp.float32)
        for d in range(n):
            out = out + recv[it, lax.rem(me - d + n, n)]
        for c in copies:
            c.wait_send()
        return out

    log_scale = jnp.zeros((1, LANES), jnp.float32)
    for it in range(ITERS):
        t = total(it, sums(log_scale, True))
        crossed, energy, traced, fisher = t[0:1], t[1:2] + EPSILON, t[2:3], t[3:4]
        effect = crossed / energy
        spread = t[4:5] - 2.0 * effect * t[5:6] + effect * effect * t[6:7]
        gradient = 0.5 * (spread - traced)
        log_scale = log_scale + jnp.tanh(gradient / (jnp.exp(log_scale) * (0.5 * fisher)))
    t = total(ITERS, sums(log_scale, False))
    z = t[0:1] / jnp.sqrt(t[1:2] + EPSILON)
    z = jnp.broadcast_to(z, (8, LANES))
    zsend[...] = z
    down = pltpu.make_async_remote_copy(
        src_ref=zsend, dst_ref=edge.at[1], send_sem=esem.at[0], recv_sem=fsem.at[1],
        device_id={"cpg": lax.max(mz - 1, 0)}, device_id_type=MESH)
    up = pltpu.make_async_remote_copy(
        src_ref=zsend, dst_ref=edge.at[0], send_sem=esem.at[1], recv_sem=fsem.at[0],
        device_id={"cpg": lax.min(mz + 1, cpgs - 1)}, device_id_type=MESH)

    @pl.when(mz > 0)
    def _():
        down.start()

    @pl.when(mz < cpgs - 1)
    def _():
        up.start()

    @pl.when(mz > 0)
    def _():
        down.wait_send()
        up.wait_recv()

    @pl.when(mz < cpgs - 1)
    def _():
        up.wait_send()
        down.wait_recv()

    lane = lax.broadcasted_iota(jnp.int32, (8, LANES), 1)
    wide = jnp.where(lane < block, z, jnp.where(lane < block + HALO, edge[1], edge[0]))
    acc = jnp.zeros((8, LANES), jnp.float32)
    norm = jnp.zeros((8, LANES), jnp.float32)
    for o in range(2 * HALO + 1):
        shift = (HALO - o) % LANES
        near = pltpu.roll(wide, shift, 1) if shift else wide
        c = band_ref[o : o + 1, :]
        acc = acc + c * near
        norm = norm + c
    row = lax.broadcasted_iota(jnp.int32, (8, LANES), 0)
    out_ref[...] = jnp.where(row == 0, acc / norm, jnp.broadcast_to(log_scale, (8, LANES)))


def fit(a, b, lam, band, n, cpgs):
    block, comps = a.shape
    fold = LANES // block
    rows = comps // fold
    big = pltpu.VMEM((rows, LANES), jnp.float32)
    return pl.pallas_call(
        functools.partial(fit_kernel, n, cpgs),
        out_shape=jax.ShapeDtypeStruct((8, LANES), jnp.float32),
        in_specs=[pl.BlockSpec(memory_space=pltpu.VMEM)] * 4,
        out_specs=pl.BlockSpec(memory_space=pltpu.VMEM),
        scratch_shapes=[
            big, big, big, big,
            pltpu.VMEM((ITERS + 1, 8, LANES), jnp.float32),
            pltpu.VMEM((ITERS + 1, n, 8, LANES), jnp.float32),
            pltpu.VMEM((2, 8, LANES), jnp.float32),
            pltpu.VMEM((8, LANES), jnp.float32),
            pltpu.SemaphoreType.DMA((ITERS + 1, n)),
            pltpu.SemaphoreType.DMA((ITERS + 1, n)),
            pltpu.SemaphoreType.DMA((2,)),
            pltpu.SemaphoreType.DMA((2,)),
        ],
        compiler_params=pltpu.CompilerParams(collective_id=1, has_side_effects=True),
        cost_estimate=pl.CostEstimate(flops=20_000_000, bytes_accessed=2_000_000, transcendentals=0),
        name="fit",
    )(a, b, lam, band)


CHUNK = 256


def rotate_kernel(n, cpgs, w_ref, d_ref, v_hbm, a_ref, b_ref, g, v, part, sent, below, above, vsem, gs, gr, ss, bs, us):
    me = lax.axis_index("samp")
    mz = lax.axis_index("cpg")
    each = w_ref.shape[0]
    total = each * n
    block = total // cpgs
    chunks = v.shape[0]
    units = 2 * chunks
    bits = [1 << i for i in range(1, n.bit_length() - 1)]
    orders = (bits, bits[::-1])
    half = w_ref.shape[1] // 2
    inputs = (w_ref, d_ref)

    def load(c):
        return pltpu.make_async_copy(v_hbm.at[:, pl.ds(pl.multiple_of(c * CHUNK, CHUNK), CHUNK)], v.at[c], vsem.at[c])

    for c in range(chunks):
        load(c).start()

    def flipped(mask):
        out = me
        bit = 1
        while bit <= mask:
            if mask & bit:
                out = out + bit - 2 * bit * lax.rem(lax.div(me, bit), 2)
            bit *= 2
        return out

    barrier = pltpu.get_barrier_semaphore()
    for bit in [1] + bits:
        pl.semaphore_signal(barrier, inc=1, device_id={"samp": flipped(bit)}, device_id_type=MESH)
    for other in (lax.rem(mz + 1, cpgs), lax.rem(mz + cpgs - 1, cpgs)):
        pl.semaphore_signal(barrier, inc=1, device_id={"cpg": other}, device_id_type=MESH)
    for k in range(2):
        g[pl.ds(pl.multiple_of(k * total + me * each, each), each), :] = inputs[k][...]
    pl.semaphore_wait(barrier, len(bits) + 3)

    def rows(k, mask):
        return pl.ds(pl.multiple_of(k * total + flipped(mask) * each, each), each)

    def hop(k, h, mask, bit):
        cols = pl.ds(h * half, half)
        dst = g.at[rows(k, mask), cols]
        return pltpu.make_async_remote_copy(
            src_ref=dst if mask else inputs[k].at[:, cols], dst_ref=dst,
            send_sem=gs.at[k, h, mask | bit], recv_sem=gr.at[k, h, mask | bit],
            device_id={"samp": flipped(bit)}, device_id_type=MESH)

    started = []

    def send(k, h, mask, bit):
        hop(k, h, mask, bit).start()
        started.append((k, h, mask, bit))

    def arrive(k, h, mask):
        cols = pl.ds(h * half, half)
        pltpu.make_async_remote_copy(
            src_ref=inputs[k].at[:, cols], dst_ref=g.at[rows(k, mask), cols],
            send_sem=gs.at[k, h, mask], recv_sem=gr.at[k, h, mask],
            device_id={"samp": flipped(1)}, device_id_type=MESH).wait_recv()

    def begin(k):
        for s in range(len(bits)):
            for h in range(2):
                send(k, h, 0, orders[h][s])
        for h in range(2):
            send(k, h, 0, 1)

    held = [[[0], [0]], [[0], [0]]]

    def relay(k, s):
        for h in range(2):
            new = [m | orders[h][s] for m in held[k][h]]
            for m in new:
                arrive(k, h, m)
                for bit in orders[h][s + 1 :]:
                    send(k, h, m, bit)
                send(k, h, m, 1)
            held[k][h] += new

    def complete(k):
        for h in range(2):
            for m in held[k][h]:
                arrive(k, h, m | 1)

    begin(0)
    for s in range(len(bits) - 1):
        relay(0, s)
    begin(1)
    relay(0, len(bits) - 1)
    complete(0)

    def hop_up(c, d):
        return pltpu.make_async_remote_copy(
            src_ref=sent.at[c, d], dst_ref=below.at[c, d], send_sem=ss.at[c, d], recv_sem=bs.at[c, d],
            device_id={"cpg": lax.min(mz + 1, cpgs - 1)}, device_id_type=MESH)

    def hop_down(c, d):
        return pltpu.make_async_remote_copy(
            src_ref=sent.at[c, d], dst_ref=above.at[c, d], send_sem=ss.at[c, d], recv_sem=us.at[c, d],
            device_id={"cpg": lax.max(mz - 1, 0)}, device_id_type=MESH)

    def own(u, d):
        return part[u, pl.ds(pl.multiple_of(d * block, block), block), :]

    def pass_on(c, d, hop_of, landed, first):
        @pl.when(first)
        def _():
            sent[c, d] = own(c, d).astype(jnp.bfloat16)

        @pl.when(jnp.logical_not(first))
        def _():
            hop_of(c, d).wait_recv()
            sent[c, d] = (own(c, d) + landed[c, d].astype(jnp.float32)).astype(jnp.bfloat16)

        hop_of(c, d).start()

    def turn(t, carry):
        for s in range(len(bits) - 1):
            @pl.when(t == chunks * (s + 1) // len(bits) - 1)
            def _():
                relay(1, s)

        @pl.when(t == chunks)
        def _():
            relay(1, len(bits) - 1)
            complete(1)

        @pl.when(t < chunks)
        def _():
            load(t).wait()

        @pl.when(t < units)
        def _():
            k = lax.div(t, chunks)
            left = g[pl.ds(pl.multiple_of(k * total, total), total), :]
            part[t] = jnp.dot(left, v[t - k * chunks], preferred_element_type=jnp.float32)

        cu = t - mz

        @pl.when((cu >= 0) & (cu < units))
        def _():
            def body(i, carry):
                pass_on(cu, cpgs - 1 - i, hop_up, below, mz == 0)
                return carry

            lax.fori_loop(0, cpgs - 1 - mz, body, 0)

        cd = t - (cpgs - 1 - mz)

        @pl.when((cd >= 0) & (cd < units))
        def _():
            def body(i, carry):
                pass_on(cd, i, hop_down, above, mz == cpgs - 1)
                return carry

            lax.fori_loop(0, mz, body, 0)

        return carry

    lax.fori_loop(0, units + cpgs - 1, turn, 0)

    def finish(c, carry):
        cols = pl.ds(pl.multiple_of(c * CHUNK, CHUNK), CHUNK)
        for k, out in enumerate((a_ref, b_ref)):
            u = k * chunks + c
            out[:, cols] = own(u, mz)

            @pl.when(mz > 0)
            def _():
                hop_up(u, mz).wait_recv()
                out[:, cols] += below[u, mz].astype(jnp.float32)

            @pl.when(mz < cpgs - 1)
            def _():
                hop_down(u, mz).wait_recv()
                out[:, cols] += above[u, mz].astype(jnp.float32)

        return carry

    lax.fori_loop(0, chunks, finish, 0)

    def drain(c, carry):
        for d in range(cpgs):
            @pl.when(d != mz)
            def _():
                hop_up(c, d).wait_send()
        return carry

    lax.fori_loop(0, units, drain, 0)
    for item in started:
        hop(*item).wait_send()


def rotate(weighted, design, eigvecs, n, cpgs):
    each, samples = weighted.shape
    comps = eigvecs.shape[1]
    total = each * n
    block = total // cpgs
    chunks = comps // CHUNK
    travel = pltpu.VMEM((2 * chunks, cpgs, block, CHUNK), jnp.bfloat16)
    piece = pltpu.SemaphoreType.DMA((2 * chunks, cpgs))
    out = jax.ShapeDtypeStruct((block, comps), jnp.float32)
    vmem = pl.BlockSpec(memory_space=pltpu.VMEM)
    return pl.pallas_call(
        functools.partial(rotate_kernel, n, cpgs),
        out_shape=(out, out),
        in_specs=[vmem, vmem, pl.BlockSpec(memory_space=pl.ANY)],
        out_specs=(vmem, vmem),
        scratch_shapes=[
            pltpu.VMEM((2 * total, samples), jnp.bfloat16),
            pltpu.VMEM((chunks, samples, CHUNK), jnp.bfloat16),
            pltpu.VMEM((2 * chunks, total, CHUNK), jnp.float32),
            travel, travel, travel,
            pltpu.SemaphoreType.DMA((chunks,)),
            pltpu.SemaphoreType.DMA((2, 2, n)),
            pltpu.SemaphoreType.DMA((2, 2, n)),
            piece, piece, piece,
        ],
        compiler_params=pltpu.CompilerParams(collective_id=2, has_side_effects=True, vmem_limit_bytes=60 * 1024 * 1024),
        cost_estimate=pl.CostEstimate(flops=4 * total * samples * comps, bytes_accessed=2 * samples * comps, transcendentals=0),
        name="rotate",
    )(weighted, design, eigvecs)


def band_of(positions, reaches):
    block = reaches.shape[0]
    total = block * lax.axis_size("cpg")
    base = lax.axis_index("cpg") * block
    places = lax.dynamic_slice_in_dim(jnp.pad(positions.astype(jnp.float32), HALO), base, block + 2 * HALO, 0)
    centre = places[HALO : HALO + block]
    index = jnp.arange(2 * HALO + 1, dtype=jnp.int32)[:, None] + jnp.arange(block, dtype=jnp.int32)[None, :]
    near = jnp.stack([places[o : o + block] for o in range(2 * HALO + 1)])
    at = index + base - HALO
    offset = jnp.abs(jnp.arange(2 * HALO + 1, dtype=jnp.int32) - HALO)[:, None]
    keep = (at >= 0) & (at < total) & (offset <= reaches[None, :])
    band = jnp.where(keep, jnp.exp(-jnp.abs(near - centre[None, :]) / band_width), 0.0)
    return jnp.pad(band, ((0, 7), (0, LANES - block)), constant_values=0.0)


def shards(responses, weights, phenotype, eigvecs, eigvals, positions, reaches):
    root_weight = jnp.sqrt(weights.astype(jnp.float32))
    weighted = (root_weight * responses.astype(jnp.float32)).astype(jnp.bfloat16)
    design = (root_weight * phenotype[None, :]).astype(jnp.bfloat16)

    n, cpgs = lax.axis_size("samp"), lax.axis_size("cpg")
    rot_resp, rot_design = rotate(weighted, design, eigvecs, n, cpgs)
    out = fit(rot_resp, rot_design, eigvals[None, :], band_of(positions, reaches), n, cpgs)
    block = reaches.shape[0]
    return (out[0, :block], out[1, :block])


def solution(mesh):
    in_specs = (P("samp", "cpg"), P("samp", "cpg"), P("cpg"), P("cpg", "samp"), P("samp"), P(), P("cpg"))
    out_specs = (P("cpg"), P("cpg"))
    return jax.shard_map(shards, mesh=mesh, in_specs=in_specs, out_specs=out_specs, check_vma=False)
```

profile of v0, /device:TPU:0, one launch (start us, length us, event | category | flops | bytes accessed | tf_op | source)
XLA Modules:
  0.0 95.7 jit_solution(12622374280202107511)
XLA Ops:
  0.6 0.0 copy-start
  0.6 0.0 copy-start.1
  0.7 2.1 %multiply_convert_fusion = (bf16[32,4096]{1,0:T(8,128)(2,1)}, bf16[32,4096]{1,0:T(8,128)(2,1)}) fusion(bf16[32,4096]{1,0:T(8,128)(2,1)} %param.8, f32[4096]{0:T(1024)} %param.9, bf16[32,4096]{1,0:T(8,128)(2,1)} %param.7), kind=kLoop, calls=%fused_computation | loop fusion | flops 786432 | bytes 1064960 | tf_op jit(solution)/shard_map/convert_element_type | solution.py:422
  2.7 66.2 %rotate.1 = (f32[64,2048]{1,0:T(8,128)}, f32[64,2048]{1,0:T(8,128)}) custom-call(bf16[32,4096]{1,0:T(8,128)(2,1)} %get-tuple-element.7.w_ref, bf16[32,4096]{1,0:T(8,128)(2,1)} %get-tuple-element.6.d_ref, bf16[4096,2048]{1,0:T(8,128)(2,1)} %v_hbm.1), custom_call_target="tpu_custom_call" | custom-call | flops 8589934592 | bytes 16777216 | tf_op jit(solution)/shard_map/rotate/pallas_call | solution.py:383
  68.9 0.0 copy-done
  68.9 0.1 pad_dynamic-slice_fusion
  69.0 0.1 fusion.4
  69.1 0.1 stack.71
  69.2 0.0 copy-done.1
  69.2 0.1 exponential_select_fusion
  69.3 0.6 pad.9.band_ref
  69.9 24.6 %fit.1 = f32[8,128]{1,0:T(8,128)} custom-call(f32[64,2048]{1,0:T(8,128)} %get-tuple-element.4.a_ref, f32[64,2048]{1,0:T(8,128)} %get-tuple-element.5.b_ref, f32[1,2048]{1,0:T(1,128)} %bitcast.39, f32[24,128]{1,0:T(8,128)} %pad.9.band_ref), custom_call_target="tpu_custom_call" | custom-call | flops 20000000 | bytes 2000000 | tf_op jit(solution)/shard_map/fit/pallas_call | solution.py:154
  94.4 1.3 %slice_bitcast_fusion = (f32[64]{0:T(128)}, f32[64]{0:T(128)}) fusion(f32[8,128]{1,0:T(8,128)} %fit.1), kind=kLoop, calls=%fused_computation.10 | loop fusion | bytes 1024 | tf_op jit(solution)/shard_map/squeeze | solution.py:428
  (2 shorter events, 0.0 us)
Async XLA Ops:
  0.6 68.3 %copy-start = (s32[256]{0:T(256)S(1)}, s32[256]{0:T(256)}, u32[]{:S(2)}) copy-start(s32[256]{0:T(256)} %param.12) | copy-start | bytes 3076
  0.6 68.5 %copy-start.1 = (s32[64]{0:T(128)S(1)}, s32[64]{0:T(128)}, u32[]{:S(2)}) copy-start(s32[64]{0:T(128)} %param.13) | copy-start | bytes 772
where the time goes:
time: 95.9 us; the launch traced here: 95.7 us
  Pallas kernels  90.7 us (95%)
  other arithmetic  2.15 us (2%)
  local copies, waits for them, and re-layouts  2.13 us (2%)
    pallas_call x1, Pallas kernels, rotate(): pl.pallas_call(functools.partial(rotate_kernel, n, cpgs), out_shape=(out,...  66.2 us
    pallas_call x1, Pallas kernels, fit(): pl.pallas_call(functools.partial(fit_kernel, n, cpgs), out_shape=jax.Shap...  24.6 us
    convert_element_type x1, other arithmetic, shards(): design = (root_weight * phenotype[None, :]).astype(jnp.bfloat16)  2.07 us

commit v1 on v0

v1 whole, which is shorter than its diff:
```python
import functools

import jax
import jax.numpy as jnp
from jax import lax
from jax.experimental import pallas as pl
from jax.experimental.pallas import tpu as pltpu
from jax.sharding import PartitionSpec as P

ITERS = 4
HALO = 8
EPSILON = 1e-06
band_width = 1000.0
MESH = pl.DeviceIdType.MESH
LANES = 128
CHUNK = 256
SKEW = 4
STRIP = 512


def score_kernel(n, cpgs, w_hbm, r_hbm, ph_ref, v_hbm, lam_ref, pos_ref, reach_ref, out_ref,
                 wbuf, rbuf, g, v, part, sent, landed, full, pp, qq, rr, lb, lamg, mail, got, pad, band,
                 wsem, vsem, gs, gr, ls, lr, zs, zr, hs, hr, es, er, bs, br):
    me = lax.axis_index("samp")
    mz = lax.axis_index("cpg")
    last = cpgs - 1
    each, samples = wbuf.shape
    half = each // 2
    pair = 2 * half
    side = 2 * pair
    phases = g.shape[0]
    chunks = v.shape[0]
    units = phases * chunks
    total = each * n
    block = total // cpgs
    bits = [1 << i for i in range(1, n.bit_length() - 1)]
    orders = (bits, bits[::-1])
    pieces = gs.shape[2]
    cols = samples // pieces
    is_end = (mz == 0) | (mz == last)

    def mask_of(h, j):
        return sum(bit for i, bit in enumerate(orders[h]) if (j >> i) & 1)

    def flipped(mask):
        out = me
        bit = 1
        while bit <= mask:
            if mask & bit:
                out = out + bit - 2 * bit * lax.rem(lax.div(me, bit), 2)
            bit *= 2
        return out

    loads = [pltpu.make_async_copy(w_hbm, wbuf, wsem.at[0]), pltpu.make_async_copy(r_hbm, rbuf, wsem.at[1])]
    for c in loads:
        c.start()

    def load(c):
        return pltpu.make_async_copy(v_hbm.at[:, pl.ds(pl.multiple_of(c * CHUNK, CHUNK), CHUNK)], v.at[c], vsem.at[c])

    for c in range(chunks):
        load(c).start()

    got[...] = jnp.zeros_like(got)
    barrier = pltpu.get_barrier_semaphore()
    for j in range(1, n):
        pl.semaphore_signal(barrier, inc=1, device_id={"samp": flipped(j)}, device_id_type=MESH)

    @pl.when(mz > 0)
    def _():
        pl.semaphore_signal(barrier, inc=1, device_id={"cpg": lax.max(mz - 1, 0)}, device_id_type=MESH)

    @pl.when(mz < last)
    def _():
        pl.semaphore_signal(barrier, inc=1, device_id={"cpg": lax.min(mz + 1, last)}, device_id_type=MESH)

    for c in loads:
        c.wait()

    def rows_of(h, cb):
        return pl.ds(h * side + cb * pair, pair)

    def prepare(i, carry):
        at = pl.ds(pl.multiple_of(i * STRIP, STRIP), STRIP)
        root = jnp.sqrt(wbuf[:, at].astype(jnp.float32))
        weighted = (root * rbuf[:, at].astype(jnp.float32)).astype(jnp.bfloat16)
        design = (root * ph_ref[:, at]).astype(jnp.bfloat16)
        for h in range(2):
            g[0, pl.ds(h * side, half), at] = weighted[h * half : (h + 1) * half]
            g[0, pl.ds(h * side + half, half), at] = design[h * half : (h + 1) * half]
        return carry

    lax.fori_loop(0, samples // STRIP, prepare, 0)

    def piece(q):
        return pl.ds(pl.multiple_of(q * cols, cols), cols)

    def ship(h, src, dst, q, bit):
        return pltpu.make_async_remote_copy(
            src_ref=g.at[src, rows_of(h, 0), piece(q)], dst_ref=g.at[dst, rows_of(h, 0), piece(q)],
            send_sem=gs.at[h, dst, q], recv_sem=gr.at[h, dst, q],
            device_id={"samp": flipped(bit)}, device_id_type=MESH)

    def share(h, j, q):
        return pltpu.make_async_remote_copy(
            src_ref=g.at[j, rows_of(h, 0), piece(q)], dst_ref=g.at[j, rows_of(h, 1), piece(q)],
            send_sem=ls.at[h, j, q], recv_sem=lr.at[h, j, q],
            device_id={"samp": flipped(1)}, device_id_type=MESH)

    pl.semaphore_wait(barrier, n - 1 + (mz > 0).astype(jnp.int32) + (mz < last).astype(jnp.int32))

    for q in range(pieces):
        for h in range(2):
            ship(h, 0, 1, q, orders[h][0]).start()
    for q in range(pieces):
        for h in range(2):
            share(h, 0, q).start()
    for i in range(1, len(bits)):
        for q in range(pieces):
            for h in range(2):
                ship(h, 0, 1 << i, q, orders[h][i]).start()

    lane = lax.broadcasted_iota(jnp.int32, (8, LANES), 1)

    def spread_out(cur, before, after):
        right = pltpu.roll(after, block, 1)
        left = pltpu.roll(before, LANES - block, 1)
        return jnp.where(lane < block, cur, jnp.where(lane < block + HALO, right, left))

    def spots(b):
        at = b * block
        row = pos_ref[0:1, pl.ds(pl.multiple_of(lax.div(at, LANES) * LANES, LANES), LANES)].astype(jnp.float32)
        return pltpu.roll(jnp.broadcast_to(row, (8, LANES)), lax.rem(LANES - lax.rem(at, LANES), LANES), 1)

    pad[...] = jnp.zeros_like(pad)
    pad[0:1, 0:block] = reach_ref[...]
    reach = jnp.broadcast_to(pad[0:1, :], (8, LANES))
    places = spread_out(spots(mz), spots(lax.max(mz - 1, 0)), spots(lax.min(mz + 1, last)))
    norm = jnp.zeros((8, LANES), jnp.float32)
    for o in range(2 * HALO + 1):
        shift = (HALO - o) % LANES
        near = pltpu.roll(places, shift, 1) if shift else places
        at = mz * block + lane + (o - HALO)
        keep = (at >= 0) & (at < total) & (abs(o - HALO) <= reach)
        c = jnp.where(keep, jnp.exp(-jnp.abs(near - places) / band_width), 0.0)
        band[o] = c
        norm = norm + c
    band[2 * HALO + 1] = jnp.where(lane < block, norm, 1.0)
    lamg[0] = lam_ref[...]

    def greet(mask):
        return pltpu.make_async_remote_copy(
            src_ref=lam_ref, dst_ref=lamg.at[mask], send_sem=es.at[mask], recv_sem=er.at[mask],
            device_id={"samp": flipped(mask)}, device_id_type=MESH)

    def chain(d, i):
        return pltpu.make_async_remote_copy(
            src_ref=sent.at[d, i], dst_ref=landed.at[d, i], send_sem=zs.at[d, i], recv_sem=zr.at[d, i],
            device_id={"cpg": lax.min(mz + 1, last) if d else lax.max(mz - 1, 0)}, device_id_type=MESH)

    def hand(d, j, c, cb):
        slot = mask_of(d, j) | cb
        return pltpu.make_async_remote_copy(
            src_ref=sent.at[d, j * chunks + c, pl.ds(cb * pair, pair)], dst_ref=full.at[slot, c],
            send_sem=hs.at[j * chunks + c, cb], recv_sem=hr.at[slot, c],
            device_id={"samp": flipped(slot)}, device_id_type=MESH)

    def deliver(d, i):
        for j in range(phases):
            @pl.when(lax.div(i, chunks) == j)
            def _():
                c = i - j * chunks
                if j == 0:
                    full[0, c] = sent[d, i, 0:pair, :]
                    hand(d, 0, c, 1).start()
                elif j == phases - 1:
                    for cb in range(2):
                        hand(d, j, c, cb).start()
                elif j == phases - 2:
                    for held in range(1, phases - 1):
                        for cb in range(2):
                            hand(d, held, c, cb).start()

    def advance(d, i, first, end):
        own = part[i, pl.ds(d * side, side), :]

        @pl.when(first)
        def _():
            sent[d, i] = own.astype(jnp.bfloat16)

        @pl.when(jnp.logical_not(first))
        def _():
            chain(d, i).wait_recv()
            sent[d, i] = (own + landed[d, i].astype(jnp.float32)).astype(jnp.bfloat16)

        @pl.when(jnp.logical_not(end))
        def _():
            chain(d, i).start()

        @pl.when(end)
        def _():
            deliver(d, i)

    def turn(t, carry):
        j = lax.div(t, chunks)
        c = t - j * chunks

        @pl.when(t < chunks)
        def _():
            load(c).wait()

        @pl.when((c == 0) & (t < units))
        def _():
            for q in range(pieces):
                for h in range(2):
                    share(h, j, q).wait_recv()

        @pl.when((t == (phases - 1) * chunks) & is_end)
        def _():
            for mask in range(1, n):
                greet(mask).start()

        @pl.when(t < units)
        def _():
            part[t] = jnp.dot(g[j], v[c], preferred_element_type=jnp.float32)

        up = t - SKEW * mz

        @pl.when((up >= 0) & (up < units))
        def _():
            advance(1, up, mz == 0, mz == last)

        down = t - SKEW * (last - mz)

        @pl.when((down >= 0) & (down < units))
        def _():
            advance(0, down, mz == last, mz == 0)

        q = lax.div(c, 2)
        for nxt in range(1, phases):
            for h in range(2):
                @pl.when((j == nxt - 1) & (lax.rem(c, 2) == h))
                def _():
                    top = nxt.bit_length() - 1
                    ship(h, nxt - (1 << top), nxt, q, orders[h][top]).wait_recv()
                    share(h, nxt, q).start()
                    for i in range(top + 1, len(bits)):
                        ship(h, nxt, nxt | (1 << i), q, orders[h][i]).start()

        return carry

    lax.fori_loop(0, units + SKEW * last, turn, 0)

    row = lax.broadcasted_iota(jnp.int32, (half, LANES), 0)
    lane_of = lax.broadcasted_iota(jnp.int32, (half, LANES), 1)
    which = (mz == last).astype(jnp.int32)
    base = me * each + which * half
    home = lax.div(base, block)
    slot_mine = which * n + me

    def post(step, i):
        return pltpu.make_async_remote_copy(
            src_ref=mail, dst_ref=got.at[slot_mine], send_sem=bs.at[step, i], recv_sem=br.at[slot_mine],
            device_id={"samp": lax.rem(me + i, n), "cpg": lax.clamp(0, home + step - 1, last)}, device_id_type=MESH)

    def each_post(act):
        for step in range(3):
            plane = home + step - 1

            @pl.when((plane >= 0) & (plane <= last))
            def _():
                def body(i, carry):
                    @pl.when((i > 0) | (plane != mz))
                    def _():
                        act(post(step, i))
                    return carry

                lax.fori_loop(0, n, body, 0)

    def fold(x):
        return sum(x[:, k * LANES : (k + 1) * LANES] for k in range(CHUNK // LANES))

    def tall(x):
        return jnp.concatenate([x] * (half // 8), axis=0)

    def settle(acc):
        return [jnp.sum(x, axis=1, keepdims=True) for x in acc]

    def newton(log_scale, acc):
        crossed, energy, traced, fisher, s_r, s_p, s_q = settle(acc)
        effect = crossed / (energy + EPSILON)
        spread = s_r - 2.0 * effect * s_p + effect * effect * s_q
        gradient = 0.5 * (spread - traced)
        return log_scale + jnp.tanh(gradient / (jnp.exp(log_scale) * (0.5 * fisher)))

    @pl.when(is_end)
    def _():
        acc = tuple(jnp.zeros((half if k < 5 else 8, LANES), jnp.float32) for k in range(7))
        for j in range(phases):
            for cb in range(2):
                here = j == 0 and cb == 0
                slot = jnp.where(mz == 0, mask_of(0, j) + cb, mask_of(1, j) + cb)

                if not here:
                    pltpu.make_async_remote_copy(
                        src_ref=lam_ref, dst_ref=lamg.at[slot], send_sem=es.at[slot], recv_sem=er.at[slot],
                        device_id={"samp": flipped(1)}, device_id_type=MESH).wait_recv()

                def absorb(c, acc):
                    if not here:
                        pltpu.make_async_remote_copy(
                            src_ref=sent.at[0, 0, pl.ds(0, pair)], dst_ref=full.at[slot, c],
                            send_sem=hs.at[0, 0], recv_sem=hr.at[slot, c],
                            device_id={"samp": flipped(1)}, device_id_type=MESH).wait_recv()
                    at = slot * chunks + c
                    a = full[slot, c, 0:half, :].astype(jnp.float32)
                    b = full[slot, c, half:pair, :].astype(jnp.float32)
                    p, q, r = a * b, b * b, a * a
                    pp[at] = p
                    qq[at] = q
                    rr[at] = r
                    lam = lamg[slot, 0:1, pl.ds(pl.multiple_of(c * CHUNK, CHUNK), CHUNK)]
                    lam = jnp.broadcast_to(lam, (8, CHUNK))
                    lb[at] = lam
                    inv = 1.0 / (lam + 1.0)
                    lev = lam * inv
                    s = tall(lev * inv)
                    inv = tall(inv)
                    terms = (p * inv, q * inv, s * r, s * p, s * q, lev, lev * lev)
                    return tuple(x + fold(y) for x, y in zip(acc, terms))

                acc = lax.fori_loop(0, chunks, absorb, acc)
        crossed, energy, s_r, s_p, s_q, traced, fisher = acc
        log_scale = newton(jnp.zeros((half, 1), jnp.float32),
                           (crossed, energy, tall(traced), tall(fisher), s_r, s_p, s_q))

        def sweep(log_scale, whole):
            scale = jnp.broadcast_to(jnp.exp(log_scale), (half, CHUNK))

            def body(i, acc):
                lam = tall(lb[i])
                inv = 1.0 / (scale * lam + 1.0)
                p = pp[i]
                q = qq[i]
                terms = [p * inv, q * inv]
                if whole:
                    lev = lam * inv
                    s = lev * inv
                    terms += [lev, lev * lev, s * rr[i], s * p, s * q]
                return tuple(x + fold(y) for x, y in zip(acc, terms))

            start = tuple(jnp.zeros((half, LANES), jnp.float32) for _ in range(7 if whole else 2))
            return lax.fori_loop(0, n * chunks, body, start)

        for _ in range(ITERS - 1):
            log_scale = newton(log_scale, sweep(log_scale, True))
        crossed, energy = settle(sweep(log_scale, False))
        zscore = crossed / jnp.sqrt(energy + EPSILON)
        hit = lane_of == row + lax.rem(base, block)
        mail[0:1, :] = jnp.sum(jnp.where(hit, jnp.broadcast_to(zscore, (half, LANES)), 0.0), axis=0, keepdims=True)
        mail[1:2, :] = jnp.sum(jnp.where(hit, jnp.broadcast_to(log_scale, (half, LANES)), 0.0), axis=0, keepdims=True)
        each_post(lambda copy: copy.start())

        @pl.when((home >= mz - 1) & (home <= mz + 1))
        def _():
            got[slot_mine] = mail[...]

    cur = jnp.zeros((2, LANES), jnp.float32)
    before = cur
    after = cur
    for h in range(2):
        for s in range(n):
            spot = (s * each + h * half) // block
            mine = (me == s) & (mz == (last if h else 0))

            @pl.when((mz >= spot - 1) & (mz <= spot + 1) & jnp.logical_not(mine))
            def _():
                pltpu.make_async_remote_copy(
                    src_ref=mail, dst_ref=got.at[h * n + s], send_sem=bs.at[0, 0], recv_sem=br.at[h * n + s],
                    device_id={"samp": flipped(1)}, device_id_type=MESH).wait_recv()

    for h in range(2):
        for s in range(n):
            spot = (s * each + h * half) // block
            value = got[h * n + s]
            cur = cur + jnp.where(mz == spot, value, 0.0)
            before = before + jnp.where(mz - 1 == spot, value, 0.0)
            after = after + jnp.where(mz + 1 == spot, value, 0.0)

    def tile(x, k):
        return jnp.broadcast_to(x[k : k + 1, :], (8, LANES))

    wide = spread_out(tile(cur, 0), tile(before, 0), tile(after, 0))
    acc = jnp.zeros((8, LANES), jnp.float32)
    for o in range(2 * HALO + 1):
        shift = (HALO - o) % LANES
        near = pltpu.roll(wide, shift, 1) if shift else wide
        acc = acc + band[o] * near
    top = lax.broadcasted_iota(jnp.int32, (8, LANES), 0)
    out_ref[...] = jnp.where(top == 0, acc / band[2 * HALO + 1], tile(cur, 1))

    def drain_gather(i, carry):
        for h in range(2):
            for j in range(phases):
                share(h, j, i).wait_send()
                if j:
                    bit = j.bit_length() - 1
                    ship(h, j - (1 << bit), j, i, orders[h][bit]).wait_send()
        return carry

    lax.fori_loop(0, pieces, drain_gather, 0)

    def drain_chain(i, carry):
        @pl.when(mz < last)
        def _():
            chain(1, i).wait_send()

        @pl.when(mz > 0)
        def _():
            chain(0, i).wait_send()
        return carry

    lax.fori_loop(0, units, drain_chain, 0)

    @pl.when(is_end)
    def _():
        for mask in range(1, n):
            greet(mask).wait_send()
        each_post(lambda copy: copy.wait_send())

        def drain_hand(c, carry):
            for j in range(phases):
                for cb in range(2):
                    if j or cb:
                        hand(0, j, c, cb).wait_send()
            return carry

        lax.fori_loop(0, chunks, drain_hand, 0)


def scores(weights, responses, phenotype, eigvecs, eigvals, positions, reaches, n, cpgs):
    each, samples = weights.shape
    comps = eigvecs.shape[1]
    chunks = comps // CHUNK
    phases = n // 2
    units = phases * chunks
    half = each // 2
    pair = 2 * half
    side = 2 * pair
    total = each * n
    pieces = max(chunks // 2, 1)
    vmem = pl.BlockSpec(memory_space=pltpu.VMEM)
    hbm = pl.BlockSpec(memory_space=pl.ANY)
    dma = pltpu.SemaphoreType.DMA
    travel = pltpu.VMEM((2, units, side, CHUNK), jnp.bfloat16)
    big = pltpu.VMEM((n * chunks, half, CHUNK), jnp.float32)
    return pl.pallas_call(
        functools.partial(score_kernel, n, cpgs),
        out_shape=jax.ShapeDtypeStruct((8, LANES), jnp.float32),
        in_specs=[hbm, hbm, vmem, hbm, vmem, vmem, vmem],
        out_specs=vmem,
        scratch_shapes=[
            pltpu.VMEM((each, samples), jnp.bfloat16),
            pltpu.VMEM((each, samples), jnp.bfloat16),
            pltpu.VMEM((phases, 2 * side, samples), jnp.bfloat16),
            pltpu.VMEM((chunks, samples, CHUNK), jnp.bfloat16),
            pltpu.VMEM((units, 2 * side, CHUNK), jnp.float32),
            travel, travel,
            pltpu.VMEM((n, chunks, pair, CHUNK), jnp.bfloat16),
            big, big, big,
            pltpu.VMEM((n * chunks, 8, CHUNK), jnp.float32),
            pltpu.VMEM((n, 1, comps), jnp.float32),
            pltpu.VMEM((2, LANES), jnp.float32),
            pltpu.VMEM((2 * n, 2, LANES), jnp.float32),
            pltpu.VMEM((8, LANES), jnp.int32),
            pltpu.VMEM((2 * HALO + 2, 8, LANES), jnp.float32),
            dma((2,)), dma((chunks,)),
            dma((2, phases, pieces)), dma((2, phases, pieces)),
            dma((2, phases, pieces)), dma((2, phases, pieces)),
            dma((2, units)), dma((2, units)),
            dma((units, 2)), dma((n, chunks)),
            dma((n,)), dma((n,)),
            dma((3, n)), dma((2 * n,)),
        ],
        compiler_params=pltpu.CompilerParams(collective_id=1, has_side_effects=True, vmem_limit_bytes=60 * 1024 * 1024),
        cost_estimate=pl.CostEstimate(flops=4 * total * samples * comps, bytes_accessed=2 * samples * comps, transcendentals=0),
        name="scores",
    )(weights, responses, phenotype[None, :], eigvecs, eigvals[None, :], positions[None, :], reaches[None, :])


def shards(responses, weights, phenotype, eigvecs, eigvals, positions, reaches):
    n, cpgs = lax.axis_size("samp"), lax.axis_size("cpg")
    out = scores(weights, responses, phenotype, eigvecs, eigvals, positions, reaches, n, cpgs)
    block = reaches.shape[0]
    return (out[0, :block], out[1, :block])


def solution(mesh):
    in_specs = (P("samp", "cpg"), P("samp", "cpg"), P("cpg"), P("cpg", "samp"), P("samp"), P(), P("cpg"))
    out_specs = (P("cpg"), P("cpg"))
    return jax.shard_map(shards, mesh=mesh, in_specs=in_specs, out_specs=out_specs, check_vma=False)
```

time: 95.9 us -> 68 us (0.71)
  Pallas kernels: 90.7 us -> 65.8 us
  other arithmetic: 2.15 us -> 0 us
    pallas_call x2 -> x1, Pallas kernels: 90.7 us -> 65.8 us  [scores(): pl.pallas_call(functools.partial(score_kernel, n, cpgs), out_shape=jax.Sh...]
    convert_element_type x2 -> x0, other arithmetic: 2.07 us -> none  [the longest x1 2.07 us: shards(): design = (root_weight * phenotype[None, :]).astype(jnp.bfloat16)]
where the time goes in v1:
time: 68 us; the launch traced here: 67.7 us
  Pallas kernels  65.8 us (97%)
  local copies, waits for them, and re-layouts  1.26 us (2%)
    pallas_call x1, Pallas kernels, scores(): pl.pallas_call(functools.partial(score_kernel, n, cpgs), out_shape=jax.Sh...  65.8 us

profile of v1, /device:TPU:0, one launch (start us, length us, event | category | flops | bytes accessed | tf_op | source)
XLA Modules:
  0.0 67.7 jit_solution(3201804912033184738)
XLA Ops:
  0.6 65.8 %scores.1 = f32[8,128]{1,0:T(8,128)} custom-call(bf16[32,4096]{1,0:T(8,128)(2,1)} %w_hbm.1, bf16[32,4096]{1,0:T(8,128)(2,1)} %r_hbm.1, f32[1,4096]{1,0:T(1,128)} %bitcast.8, bf16[4096,2048]{1,0:T(8,128)(2,1)} %v_hbm.1, f32[1,2048]{1,0:T(1,128)} %bitcast.9, s32[1,256]{1,0:T(1,128)} %bitcast.10, s32[1,64]{1,0:T(1,128)} %bitcast.11), custom_call_target="tpu_custom_call" | custom-call | flops 8589934592 | bytes 16777216 | tf_op jit(solution)/shard_map/scores/pallas_call | solution.py:457
  66.5 1.3 %slice_bitcast_fusion = (f32[64]{0:T(128)}, f32[64]{0:T(128)}) fusion(f32[8,128]{1,0:T(8,128)} %scores.1), kind=kLoop, calls=%fused_computation | loop fusion | bytes 1024 | tf_op jit(solution)/shard_map/squeeze | solution.py:495

commit v2 on v1

--- a/solution.py
+++ b/solution.py
@@ -16,6 +16,8 @@
 CHUNK = 256
 SKEW = 4
 STRIP = 512
+AHEAD = 3
+UNROLL = 4
 
 
 def score_kernel(n, cpgs, w_hbm, r_hbm, ph_ref, v_hbm, lam_ref, pos_ref, reach_ref, out_ref,
@@ -35,7 +37,7 @@
     block = total // cpgs
     bits = [1 << i for i in range(1, n.bit_length() - 1)]
     orders = (bits, bits[::-1])
-    pieces = gs.shape[2]
+    pieces = gr.shape[2]
     cols = samples // pieces
     is_end = (mz == 0) | (mz == last)
 
@@ -58,9 +60,6 @@
     def load(c):
         return pltpu.make_async_copy(v_hbm.at[:, pl.ds(pl.multiple_of(c * CHUNK, CHUNK), CHUNK)], v.at[c], vsem.at[c])
 
-    for c in range(chunks):
-        load(c).start()
-
     got[...] = jnp.zeros_like(got)
     barrier = pltpu.get_barrier_semaphore()
     for j in range(1, n):
@@ -74,8 +73,11 @@
     def _():
         pl.semaphore_signal(barrier, inc=1, device_id={"cpg": lax.min(mz + 1, last)}, device_id_type=MESH)
 
-    for c in loads:
-        c.wait()
+    with jax.named_scope("loadwait"):
+        for c in loads:
+            c.wait()
+    for c in range(min(AHEAD, chunks)):
+        load(c).start()
 
     def rows_of(h, cb):
         return pl.ds(h * side + cb * pair, pair)
@@ -90,7 +92,8 @@
             g[0, pl.ds(h * side + half, half), at] = design[h * half : (h + 1) * half]
         return carry
 
-    lax.fori_loop(0, samples // STRIP, prepare, 0)
+    with jax.named_scope("prep"):
+        lax.fori_loop(0, samples // STRIP, prepare, 0)
 
     def piece(q):
         return pl.ds(pl.multiple_of(q * cols, cols), cols)
@@ -98,13 +101,13 @@
     def ship(h, src, dst, q, bit):
         return pltpu.make_async_remote_copy(
             src_ref=g.at[src, rows_of(h, 0), piece(q)], dst_ref=g.at[dst, rows_of(h, 0), piece(q)],
-            send_sem=gs.at[h, dst, q], recv_sem=gr.at[h, dst, q],
+            send_sem=gs.at[h], recv_sem=gr.at[h, dst, q],
             device_id={"samp": flipped(bit)}, device_id_type=MESH)
 
     def share(h, j, q):
         return pltpu.make_async_remote_copy(
             src_ref=g.at[j, rows_of(h, 0), piece(q)], dst_ref=g.at[j, rows_of(h, 1), piece(q)],
-            send_sem=ls.at[h, j, q], recv_sem=lr.at[h, j, q],
+            send_sem=ls.at[h], recv_sem=lr.at[h, j],
             device_id={"samp": flipped(1)}, device_id_type=MESH)
 
     pl.semaphore_wait(barrier, n - 1 + (mz > 0).astype(jnp.int32) + (mz < last).astype(jnp.int32))
@@ -115,10 +118,14 @@
     for q in range(pieces):
         for h in range(2):
             share(h, 0, q).start()
-    for i in range(1, len(bits)):
-        for q in range(pieces):
-            for h in range(2):
-                ship(h, 0, 1 << i, q, orders[h][i]).start()
+
+    def shared(h, j):
+        return pltpu.make_async_remote_copy(
+            src_ref=g.at[j, rows_of(h, 0)], dst_ref=g.at[j, rows_of(h, 1)], send_sem=ls.at[h], recv_sem=lr.at[h, j],
+            device_id={"samp": flipped(1)}, device_id_type=MESH)
+
+    def top_of(j):
+        return j.bit_length() - 1
 
     lane = lax.broadcasted_iota(jnp.int32, (8, LANES), 1)
 
@@ -150,23 +157,23 @@
 
     def greet(mask):
         return pltpu.make_async_remote_copy(
-            src_ref=lam_ref, dst_ref=lamg.at[mask], send_sem=es.at[mask], recv_sem=er.at[mask],
+            src_ref=lam_ref, dst_ref=lamg.at[mask], send_sem=es.at[0], recv_sem=er.at[0],
             device_id={"samp": flipped(mask)}, device_id_type=MESH)
 
     def chain(d, i):
         return pltpu.make_async_remote_copy(
-            src_ref=sent.at[d, i], dst_ref=landed.at[d, i], send_sem=zs.at[d, i], recv_sem=zr.at[d, i],
+            src_ref=sent.at[d, i], dst_ref=landed.at[d, i], send_sem=zs.at[d], recv_sem=zr.at[d, i],
             device_id={"cpg": lax.min(mz + 1, last) if d else lax.max(mz - 1, 0)}, device_id_type=MESH)
 
     def hand(d, j, c, cb):
         slot = mask_of(d, j) | cb
         return pltpu.make_async_remote_copy(
             src_ref=sent.at[d, j * chunks + c, pl.ds(cb * pair, pair)], dst_ref=full.at[slot, c],
-            send_sem=hs.at[j * chunks + c, cb], recv_sem=hr.at[slot, c],
+            send_sem=hs.at[0], recv_sem=hr.at[slot],
             device_id={"samp": flipped(slot)}, device_id_type=MESH)
 
-    def deliver(d, i):
-        for j in range(phases):
+    def deliver(d, i, options):
+        for j in options:
             @pl.when(lax.div(i, chunks) == j)
             def _():
                 c = i - j * chunks
@@ -181,86 +188,104 @@
                         for cb in range(2):
                             hand(d, held, c, cb).start()
 
-    def advance(d, i, first, end):
-        own = part[i, pl.ds(d * side, side), :]
+    def advance(d, i, first, end, options):
+        def own():
+            return part[i, pl.ds(d * side, side), :]
 
         @pl.when(first)
         def _():
-            sent[d, i] = own.astype(jnp.bfloat16)
+            sent[d, i] = own().astype(jnp.bfloat16)
+            chain(d, i).start()
 
         @pl.when(jnp.logical_not(first))
         def _():
             chain(d, i).wait_recv()
-            sent[d, i] = (own + landed[d, i].astype(jnp.float32)).astype(jnp.bfloat16)
-
-        @pl.when(jnp.logical_not(end))
-        def _():
-            chain(d, i).start()
-
-        @pl.when(end)
-        def _():
-            deliver(d, i)
-
-    def turn(t, carry):
-        j = lax.div(t, chunks)
-        c = t - j * chunks
-
-        @pl.when(t < chunks)
-        def _():
-            load(c).wait()
-
-        @pl.when((c == 0) & (t < units))
-        def _():
-            for q in range(pieces):
+            sent[d, i] = (own() + landed[d, i].astype(jnp.float32)).astype(jnp.bfloat16)
+
+            @pl.when(jnp.logical_not(end))
+            def _():
+                chain(d, i).start()
+
+            if options:
+                @pl.when(end)
+                def _():
+                    deliver(d, i, options)
+
+    lag = SKEW * last
+
+    def forward(t, low, high):
+        options = [j for j in range(phases) if low - lag < (j + 1) * chunks and high - lag > j * chunks]
+        for d, behind in ((1, mz), (0, last - mz)):
+            i = t - SKEW * behind
+            with jax.named_scope("up" if d else "down"):
+                if low >= lag and high <= units:
+                    advance(d, i, behind == 0, behind == last, options)
+                else:
+                    @pl.when((i >= 0) & (i < units))
+                    def _():
+                        advance(d, i, behind == 0, behind == last, options)
+
+    def phase(j):
+        with jax.named_scope("sharewait"):
+            for h in range(2):
+                shared(h, j).wait_recv()
+        if j == phases - 1:
+            @pl.when(is_end)
+            def _():
+                for mask in range(1, n):
+                    greet(mask).start()
+
+        def step(c, carry):
+            t = j * chunks + c
+            if j == 0:
+                load(c).wait()
+
+                @pl.when(c + AHEAD < chunks)
+                def _():
+                    load(c + AHEAD).start()
+            with jax.named_scope("mm"):
+                part[t] = jnp.dot(g[j], v[c], preferred_element_type=jnp.float32)
+            forward(t, j * chunks, (j + 1) * chunks)
+            nxt = j + 1
+            if nxt < phases:
+                q = lax.div(c, 2)
                 for h in range(2):
-                    share(h, j, q).wait_recv()
-
-        @pl.when((t == (phases - 1) * chunks) & is_end)
-        def _():
-            for mask in range(1, n):
-                greet(mask).start()
-
-        @pl.when(t < units)
-        def _():
-            part[t] = jnp.dot(g[j], v[c], preferred_element_type=jnp.float32)
-
-        up = t - SKEW * mz
-
-        @pl.when((up >= 0) & (up < units))
-        def _():
-            advance(1, up, mz == 0, mz == last)
-
-        down = t - SKEW * (last - mz)
-
-        @pl.when((down >= 0) & (down < units))
-        def _():
-            advance(0, down, mz == last, mz == 0)
-
-        q = lax.div(c, 2)
-        for nxt in range(1, phases):
-            for h in range(2):
-                @pl.when((j == nxt - 1) & (lax.rem(c, 2) == h))
-                def _():
-                    top = nxt.bit_length() - 1
-                    ship(h, nxt - (1 << top), nxt, q, orders[h][top]).wait_recv()
-                    share(h, nxt, q).start()
-                    for i in range(top + 1, len(bits)):
-                        ship(h, nxt, nxt | (1 << i), q, orders[h][i]).start()
-
+                    @pl.when(lax.rem(c, 2) == h)
+                    def _():
+                        top = top_of(nxt)
+                        with jax.named_scope("shipwait"):
+                            ship(h, nxt - (1 << top), nxt, q, orders[h][top]).wait_recv()
+                        share(h, nxt, q).start()
+                        after = nxt + 1
+                        if after < phases:
+                            upper = top_of(after)
+                            turned = orders[1 - h][upper] == orders[h][top] and orders[h][upper] != orders[h][top]
+                            k = 1 - h if turned else h
+                            ship(k, after - (1 << upper), after, q, orders[k][upper]).start()
+            return carry
+
+        lax.fori_loop(0, chunks, step, 0)
+
+    for j in range(phases):
+        phase(j)
+
+    def trail(t, carry):
+        forward(t, units, units + lag)
         return carry
 
-    lax.fori_loop(0, units + SKEW * last, turn, 0)
+    lax.fori_loop(units, units + lag, trail, 0)
 
     row = lax.broadcasted_iota(jnp.int32, (half, LANES), 0)
     lane_of = lax.broadcasted_iota(jnp.int32, (half, LANES), 1)
     which = (mz == last).astype(jnp.int32)
     base = me * each + which * half
     home = lax.div(base, block)
-    slot_mine = which * n + me
+    slot_mine = 2 * me + which
+    per = block // half
 
     def post(step, i):
         return pltpu.make_async_remote_copy(
-            src_ref=mail, dst_ref=got.at[slot_mine], send_sem=bs.at[step, i], recv_sem=br.at[slot_mine],
+            src_ref=mail, dst_ref=got.at[slot_mine], send_sem=bs.at[step], recv_sem=br.at[2 - step],
             device_id={"samp": lax.rem(me + i, n), "cpg": lax.clamp(0, home + step - 1, last)}, device_id_type=MESH)
 
     def each_post(act):
@@ -295,6 +320,10 @@
 
     @pl.when(is_end)
     def _():
+        others = lamg.at[pl.ds(1, n - 1)]
+        pltpu.make_async_remote_copy(
+            src_ref=others, dst_ref=others, send_sem=es.at[0], recv_sem=er.at[0],
+            device_id={"samp": flipped(1)}, device_id_type=MESH).wait_recv()
         acc = tuple(jnp.zeros((half if k < 5 else 8, LANES), jnp.float32) for k in range(7))
         for j in range(phases):
             for cb in range(2):
@@ -303,15 +332,10 @@
 
                 if not here:
                     pltpu.make_async_remote_copy(
-                        src_ref=lam_ref, dst_ref=lamg.at[slot], send_sem=es.at[slot], recv_sem=er.at[slot],
+                        src_ref=full.at[slot], dst_ref=full.at[slot], send_sem=hs.at[0], recv_sem=hr.at[slot],
                         device_id={"samp": flipped(1)}, device_id_type=MESH).wait_recv()
 
                 def absorb(c, acc):
-                    if not here:
-                        pltpu.make_async_remote_copy(
-                            src_ref=sent.at[0, 0, pl.ds(0, pair)], dst_ref=full.at[slot, c],
-                            send_sem=hs.at[0, 0], recv_sem=hr.at[slot, c],
-                            device_id={"samp": flipped(1)}, device_id_type=MESH).wait_recv()
                     at = slot * chunks + c
                     a = full[slot, c, 0:half, :].astype(jnp.float32)
                     b = full[slot, c, half:pair, :].astype(jnp.float32)
@@ -329,7 +353,8 @@
                     terms = (p * inv, q * inv, s * r, s * p, s * q, lev, lev * lev)
                     return tuple(x + fold(y) for x, y in zip(acc, terms))
 
-                acc = lax.fori_loop(0, chunks, absorb, acc)
+                with jax.named_scope(f"absorb{2*j+cb}"):
+                    acc = lax.fori_loop(0, chunks, absorb, acc)
         crossed, energy, s_r, s_p, s_q, traced, fisher = acc
         log_scale = newton(jnp.zeros((half, 1), jnp.float32),
                            (crossed, energy, tall(traced), tall(fisher), s_r, s_p, s_q))
@@ -337,29 +362,36 @@
         def sweep(log_scale, whole):
             scale = jnp.broadcast_to(jnp.exp(log_scale), (half, CHUNK))
 
-            def body(i, acc):
+            def terms_of(i):
                 lam = tall(lb[i])
                 inv = 1.0 / (scale * lam + 1.0)
-                p = pp[i]
-                q = qq[i]
-                terms = [p * inv, q * inv]
+                p = pp[i] * inv
+                q = qq[i] * inv
+                terms = [p, q]
                 if whole:
                     lev = lam * inv
-                    s = lev * inv
-                    terms += [lev, lev * lev, s * rr[i], s * p, s * q]
-                return tuple(x + fold(y) for x, y in zip(acc, terms))
+                    terms += [lev, lev * lev, rr[i] * (lev * inv), p * lev, q * lev]
+                return [fold(y) for y in terms]
+
+            def body(i, acc):
+                for u in range(UNROLL):
+                    acc = tuple(x + y for x, y in zip(acc, terms_of(i * UNROLL + u)))
+                return acc
 
             start = tuple(jnp.zeros((half, LANES), jnp.float32) for _ in range(7 if whole else 2))
-            return lax.fori_loop(0, n * chunks, body, start)
+            return lax.fori_loop(0, n * chunks // UNROLL, body, start)
 
         for _ in range(ITERS - 1):
-            log_scale = newton(log_scale, sweep(log_scale, True))
-        crossed, energy = settle(sweep(log_scale, False))
+            with jax.named_scope("iter"):
+                log_scale = newton(log_scale, sweep(log_scale, True))
+        with jax.named_scope("lastsweep"):
+            crossed, energy = settle(sweep(log_scale, False))
         zscore = crossed / jnp.sqrt(energy + EPSILON)
         hit = lane_of == row + lax.rem(base, block)
         mail[0:1, :] = jnp.sum(jnp.where(hit, jnp.broadcast_to(zscore, (half, LANES)), 0.0), axis=0, keepdims=True)
         mail[1:2, :] = jnp.sum(jnp.where(hit, jnp.broadcast_to(log_scale, (half, LANES)), 0.0), axis=0, keepdims=True)
-        each_post(lambda copy: copy.start())
+        with jax.named_scope("post"):
+            each_post(lambda copy: copy.start())
 
         @pl.when((home >= mz - 1) & (home <= mz + 1))
         def _():
@@ -368,21 +400,29 @@
     cur = jnp.zeros((2, LANES), jnp.float32)
     before = cur
     after = cur
+
+    def letters(k, count):
+        some = got.at[pl.ds(0, count)]
+        return pltpu.make_async_remote_copy(
+            src_ref=some, dst_ref=some, send_sem=bs.at[k], recv_sem=br.at[k],
+            device_id={"samp": flipped(1)}, device_id_type=MESH)
+
+    for k in range(3):
+        near = (mz + k - 1 >= 0) & (mz + k - 1 <= last)
+        inside = is_end & (home == mz + k - 1)
+        with jax.named_scope("gotwait"):
+            @pl.when(near & inside)
+            def _():
+                letters(k, per - 1).wait_recv()
+
+            @pl.when(near & jnp.logical_not(inside))
+            def _():
+                letters(k, per).wait_recv()
+
     for h in range(2):
         for s in range(n):
             spot = (s * each + h * half) // block
-            mine = (me == s) & (mz == (last if h else 0))
-
-            @pl.when((mz >= spot - 1) & (mz <= spot + 1) & jnp.logical_not(mine))
-            def _():
-                pltpu.make_async_remote_copy(
-                    src_ref=mail, dst_ref=got.at[h * n + s], send_sem=bs.at[0, 0], recv_sem=br.at[h * n + s],
-                    device_id={"samp": flipped(1)}, device_id_type=MESH).wait_recv()
-
-    for h in range(2):
-        for s in range(n):
-            spot = (s * each + h * half) // block
-            value = got[h * n + s]
+            value = got[2 * s + h]
             cur = cur + jnp.where(mz == spot, value, 0.0)
             before = before + jnp.where(mz - 1 == spot, value, 0.0)
             after = after + jnp.where(mz + 1 == spot, value, 0.0)
@@ -399,43 +439,49 @@
     top = lax.broadcasted_iota(jnp.int32, (8, LANES), 0)
     out_ref[...] = jnp.where(top == 0, acc / band[2 * HALO + 1], tile(cur, 1))
 
-    def drain_gather(i, carry):
-        for h in range(2):
-            for j in range(phases):
-                share(h, j, i).wait_send()
-                if j:
-                    bit = j.bit_length() - 1
-                    ship(h, j - (1 << bit), j, i, orders[h][bit]).wait_send()
-        return carry
-
-    lax.fori_loop(0, pieces, drain_gather, 0)
-
-    def drain_chain(i, carry):
-        @pl.when(mz < last)
-        def _():
-            chain(1, i).wait_send()
-
-        @pl.when(mz > 0)
-        def _():
-            chain(0, i).wait_send()
-        return carry
-
-    lax.fori_loop(0, units, drain_chain, 0)
+    for h in range(2):
+        first = g.at[pl.ds(1, phases - 1), rows_of(h, 0)]
+        pltpu.make_async_remote_copy(
+            src_ref=first, dst_ref=first, send_sem=gs.at[h], recv_sem=gr.at[h, 0, 0],
+            device_id={"samp": flipped(1)}, device_id_type=MESH).wait_send()
+        every = g.at[:, rows_of(h, 0)]
+        pltpu.make_async_remote_copy(
+            src_ref=every, dst_ref=every, send_sem=ls.at[h], recv_sem=lr.at[h, 0],
+            device_id={"samp": flipped(1)}, device_id_type=MESH).wait_send()
+
+    def passed(d):
+        return pltpu.make_async_remote_copy(
+            src_ref=sent.at[d], dst_ref=landed.at[d], send_sem=zs.at[d], recv_sem=zr.at[d, 0],
+            device_id={"samp": flipped(1)}, device_id_type=MESH)
+
+    @pl.when(mz < last)
+    def _():
+        passed(1).wait_send()
+
+    @pl.when(mz > 0)
+    def _():
+        passed(0).wait_send()
 
     @pl.when(is_end)
     def _():
-        for mask in range(1, n):
-            greet(mask).wait_send()
-        each_post(lambda copy: copy.wait_send())
-
-        def drain_hand(c, carry):
-            for j in range(phases):
-                for cb in range(2):
-                    if j or cb:
-                        hand(0, j, c, cb).wait_send()
-            return carry
-
-        lax.fori_loop(0, chunks, drain_hand, 0)
+        others = lamg.at[pl.ds(1, n - 1)]
+        pltpu.make_async_remote_copy(
+            src_ref=others, dst_ref=others, send_sem=es.at[0], recv_sem=er.at[0],
+            device_id={"samp": flipped(1)}, device_id_type=MESH).wait_send()
+        handed = full.at[pl.ds(1, n - 1)]
+        pltpu.make_async_remote_copy(
+            src_ref=handed, dst_ref=handed, send_sem=hs.at[0], recv_sem=hr.at[0],
+            device_id={"samp": flipped(1)}, device_id_type=MESH).wait_send()
+        for k in range(3):
+            plane = home + k - 1
+
+            @pl.when((plane >= 0) & (plane <= last) & (plane != mz))
+            def _():
+                letters(k, n).wait_send()
+
+            @pl.when(plane == mz)
+            def _():
+                letters(k, n - 1).wait_send()
 
 
 def scores(weights, responses, phenotype, eigvecs, eigvals, positions, reaches, n, cpgs):
@@ -475,12 +521,12 @@
             pltpu.VMEM((8, LANES), jnp.int32),
             pltpu.VMEM((2 * HALO + 2, 8, LANES), jnp.float32),
             dma((2,)), dma((chunks,)),
-            dma((2, phases, pieces)), dma((2, phases, pieces)),
-            dma((2, phases, pieces)), dma((2, phases, pieces)),
-            dma((2, units)), dma((2, units)),
-            dma((units, 2)), dma((n, chunks)),
-            dma((n,)), dma((n,)),
-            dma((3, n)), dma((2 * n,)),
+            dma((2,)), dma((2, phases, pieces)),
+            dma((2,)), dma((2, phases)),
+            dma((2,)), dma((2, units)),
+            dma((1,)), dma((n,)),
+            dma((1,)), dma((1,)),
+            dma((3,)), dma((3,)),
         ],
         compiler_params=pltpu.CompilerParams(collective_id=1, has_side_effects=True, vmem_limit_bytes=60 * 1024 * 1024),
         cost_estimate=pl.CostEstimate(flops=4 * total * samples * comps, bytes_accessed=2 * samples * comps, transcendentals=0),

time: 68 us -> 57.7 us (0.85)
  Pallas kernels: 65.8 us -> 55.5 us
    pallas_call x1, Pallas kernels: 65.8 us -> 55.5 us  [scores(): pl.pallas_call(functools.partial(score_kernel, n, cpgs), out_shape=jax.Sh...]
where the time goes in v2:
time: 57.7 us; the launch traced here: 57.4 us
  Pallas kernels  55.5 us (96%)
  local copies, waits for them, and re-layouts  1.26 us (2%)
  between operations  0.64 us (1%)
    pallas_call x1, Pallas kernels, scores(): pl.pallas_call(functools.partial(score_kernel, n, cpgs), out_shape=jax.Sh...  55.5 us
    squeeze x1, local copies, waits for them, and re-layouts, shards(): return (out[0, :block], out[1, :block])  1.26 us

profile of v2, /device:TPU:0, one launch (start us, length us, event | category | flops | bytes accessed | tf_op | source)
XLA Modules:
  0.0 57.4 jit_solution(3027257678457252197)
XLA Ops:
  0.6 55.5 %scores.1 = f32[8,128]{1,0:T(8,128)} custom-call(bf16[32,4096]{1,0:T(8,128)(2,1)} %w_hbm.1, bf16[32,4096]{1,0:T(8,128)(2,1)} %r_hbm.1, f32[1,4096]{1,0:T(1,128)} %bitcast.8, bf16[4096,2048]{1,0:T(8,128)(2,1)} %v_hbm.1, f32[1,2048]{1,0:T(1,128)} %bitcast.9, s32[1,256]{1,0:T(1,128)} %bitcast.10, s32[1,64]{1,0:T(1,128)} %bitcast.11), custom_call_target="tpu_custom_call" | custom-call | flops 8589934592 | bytes 16777216 | tf_op jit(solution)/shard_map/scores/pallas_call | solution.py:503
  56.2 1.3 %slice_bitcast_fusion = (f32[64]{0:T(128)}, f32[64]{0:T(128)}) fusion(f32[8,128]{1,0:T(8,128)} %scores.1), kind=kLoop, calls=%fused_computation | loop fusion | bytes 1024 | tf_op jit(solution)/shard_map/squeeze | solution.py:541

commit v3 on v2

--- a/solution.py
+++ b/solution.py
@@ -14,14 +14,14 @@
 MESH = pl.DeviceIdType.MESH
 LANES = 128
 CHUNK = 256
-SKEW = 4
+SKEW = 5
 STRIP = 512
 AHEAD = 3
 UNROLL = 4
 
 
-def score_kernel(n, cpgs, w_hbm, r_hbm, ph_ref, v_hbm, lam_ref, pos_ref, reach_ref, out_ref,
-                 wbuf, rbuf, g, v, part, sent, landed, full, pp, qq, rr, lb, lamg, mail, got, pad, band,
+def score_kernel(n, cpgs, w_hbm, r_hbm, ph_hbm, v_hbm, lam_hbm, pos_hbm, reach_hbm, out_ref,
+                 wbuf, rbuf, g, v, part, sent, landed, full, pp, qq, rr, lb, lamg, mail, got, pad, band, ph_ref, lam_ref, pos_ref, reach_ref,
                  wsem, vsem, gs, gr, ls, lr, zs, zr, hs, hr, es, er, bs, br):
     me = lax.axis_index("samp")
     mz = lax.axis_index("cpg")
@@ -53,12 +53,13 @@
             bit *= 2
         return out
 
-    loads = [pltpu.make_async_copy(w_hbm, wbuf, wsem.at[0]), pltpu.make_async_copy(r_hbm, rbuf, wsem.at[1])]
+    moves = ((w_hbm, wbuf), (r_hbm, rbuf), (ph_hbm, ph_ref), (pos_hbm, pos_ref), (reach_hbm, reach_ref), (lam_hbm, lam_ref))
+    loads = [pltpu.make_async_copy(src, dst, wsem.at[k]) for k, (src, dst) in enumerate(moves)]
     for c in loads:
         c.start()
 
     def load(c):
-        return pltpu.make_async_copy(v_hbm.at[:, pl.ds(pl.multiple_of(c * CHUNK, CHUNK), CHUNK)], v.at[c], vsem.at[c])
+        return pltpu.make_async_copy(v_hbm.at[:, pl.ds(pl.multiple_of(c * CHUNK, CHUNK), CHUNK)], v.at[c], vsem.at[lax.rem(c, AHEAD)])
 
     got[...] = jnp.zeros_like(got)
     barrier = pltpu.get_barrier_semaphore()
@@ -74,7 +75,7 @@
         pl.semaphore_signal(barrier, inc=1, device_id={"cpg": lax.min(mz + 1, last)}, device_id_type=MESH)
 
     with jax.named_scope("loadwait"):
-        for c in loads:
+        for c in loads[:3]:
             c.wait()
     for c in range(min(AHEAD, chunks)):
         load(c).start()
@@ -101,13 +102,13 @@
     def ship(h, src, dst, q, bit):
         return pltpu.make_async_remote_copy(
             src_ref=g.at[src, rows_of(h, 0), piece(q)], dst_ref=g.at[dst, rows_of(h, 0), piece(q)],
-            send_sem=gs.at[h], recv_sem=gr.at[h, dst, q],
+            send_sem=gs.at[0], recv_sem=gr.at[h, dst - 1, q],
             device_id={"samp": flipped(bit)}, device_id_type=MESH)
 
     def share(h, j, q):
         return pltpu.make_async_remote_copy(
             src_ref=g.at[j, rows_of(h, 0), piece(q)], dst_ref=g.at[j, rows_of(h, 1), piece(q)],
-            send_sem=ls.at[h], recv_sem=lr.at[h, j],
+            send_sem=ls.at[0], recv_sem=lr.at[j],
             device_id={"samp": flipped(1)}, device_id_type=MESH)
 
     pl.semaphore_wait(barrier, n - 1 + (mz > 0).astype(jnp.int32) + (mz < last).astype(jnp.int32))
@@ -119,14 +120,17 @@
         for h in range(2):
             share(h, 0, q).start()
 
-    def shared(h, j):
-        return pltpu.make_async_remote_copy(
-            src_ref=g.at[j, rows_of(h, 0)], dst_ref=g.at[j, rows_of(h, 1)], send_sem=ls.at[h], recv_sem=lr.at[h, j],
+    def shared(j):
+        both = g.at[j, pl.ds(0, side)]
+        return pltpu.make_async_remote_copy(
+            src_ref=both, dst_ref=both, send_sem=ls.at[0], recv_sem=lr.at[j],
             device_id={"samp": flipped(1)}, device_id_type=MESH)
 
     def top_of(j):
         return j.bit_length() - 1
 
+    for c in loads[3:]:
+        c.wait()
     lane = lax.broadcasted_iota(jnp.int32, (8, LANES), 1)
 
     def spread_out(cur, before, after):
@@ -166,7 +170,7 @@
             device_id={"cpg": lax.min(mz + 1, last) if d else lax.max(mz - 1, 0)}, device_id_type=MESH)
 
     def hand(d, j, c, cb):
-        slot = mask_of(d, j) | cb
+        slot = mask_of(d, phases - 1 - j) | cb
         return pltpu.make_async_remote_copy(
             src_ref=sent.at[d, j * chunks + c, pl.ds(cb * pair, pair)], dst_ref=full.at[slot, c],
             send_sem=hs.at[0], recv_sem=hr.at[slot],
@@ -177,14 +181,11 @@
             @pl.when(lax.div(i, chunks) == j)
             def _():
                 c = i - j * chunks
-                if j == 0:
+                if j == phases - 1:
                     full[0, c] = sent[d, i, 0:pair, :]
-                    hand(d, 0, c, 1).start()
-                elif j == phases - 1:
-                    for cb in range(2):
-                        hand(d, j, c, cb).start()
-                elif j == phases - 2:
-                    for held in range(1, phases - 1):
+                    hand(d, j, c, 1).start()
+                elif j:
+                    for held in ((0, 1) if j == 1 else (j,)):
                         for cb in range(2):
                             hand(d, held, c, cb).start()
 
@@ -227,8 +228,7 @@
 
     def phase(j):
         with jax.named_scope("sharewait"):
-            for h in range(2):
-                shared(h, j).wait_recv()
+            shared(j).wait_recv()
         if j == phases - 1:
             @pl.when(is_end)
             def _():
@@ -278,9 +278,10 @@
     row = lax.broadcasted_iota(jnp.int32, (half, LANES), 0)
     lane_of = lax.broadcasted_iota(jnp.int32, (half, LANES), 1)
     which = (mz == last).astype(jnp.int32)
-    base = me * each + which * half
+    source = flipped(sum(bits))
+    base = source * each + which * half
     home = lax.div(base, block)
-    slot_mine = 2 * me + which
+    slot_mine = 2 * source + which
     per = block // half
 
     def post(step, i):
@@ -327,8 +328,8 @@
         acc = tuple(jnp.zeros((half if k < 5 else 8, LANES), jnp.float32) for k in range(7))
         for j in range(phases):
             for cb in range(2):
-                here = j == 0 and cb == 0
-                slot = jnp.where(mz == 0, mask_of(0, j) + cb, mask_of(1, j) + cb)
+                here = j == phases - 1 and cb == 0
+                slot = jnp.where(mz == 0, mask_of(0, phases - 1 - j) + cb, mask_of(1, phases - 1 - j) + cb)
 
                 if not here:
                     pltpu.make_async_remote_copy(
@@ -439,15 +440,14 @@
     top = lax.broadcasted_iota(jnp.int32, (8, LANES), 0)
     out_ref[...] = jnp.where(top == 0, acc / band[2 * HALO + 1], tile(cur, 1))
 
-    for h in range(2):
-        first = g.at[pl.ds(1, phases - 1), rows_of(h, 0)]
-        pltpu.make_async_remote_copy(
-            src_ref=first, dst_ref=first, send_sem=gs.at[h], recv_sem=gr.at[h, 0, 0],
-            device_id={"samp": flipped(1)}, device_id_type=MESH).wait_send()
-        every = g.at[:, rows_of(h, 0)]
-        pltpu.make_async_remote_copy(
-            src_ref=every, dst_ref=every, send_sem=ls.at[h], recv_sem=lr.at[h, 0],
-            device_id={"samp": flipped(1)}, device_id_type=MESH).wait_send()
+    first = g.at[pl.ds(1, phases - 1), pl.ds(0, side)]
+    pltpu.make_async_remote_copy(
+        src_ref=first, dst_ref=first, send_sem=gs.at[0], recv_sem=gr.at[0, 0, 0],
+        device_id={"samp": flipped(1)}, device_id_type=MESH).wait_send()
+    every = g.at[:, pl.ds(0, side)]
+    pltpu.make_async_remote_copy(
+        src_ref=every, dst_ref=every, send_sem=ls.at[0], recv_sem=lr.at[0],
+        device_id={"samp": flipped(1)}, device_id_type=MESH).wait_send()
 
     def passed(d):
         return pltpu.make_async_remote_copy(
@@ -503,7 +503,7 @@
     return pl.pallas_call(
         functools.partial(score_kernel, n, cpgs),
         out_shape=jax.ShapeDtypeStruct((8, LANES), jnp.float32),
-        in_specs=[hbm, hbm, vmem, hbm, vmem, vmem, vmem],
+        in_specs=[hbm] * 7,
         out_specs=vmem,
         scratch_shapes=[
             pltpu.VMEM((each, samples), jnp.bfloat16),
@@ -520,9 +520,13 @@
             pltpu.VMEM((2 * n, 2, LANES), jnp.float32),
             pltpu.VMEM((8, LANES), jnp.int32),
             pltpu.VMEM((2 * HALO + 2, 8, LANES), jnp.float32),
-            dma((2,)), dma((chunks,)),
-            dma((2,)), dma((2, phases, pieces)),
-            dma((2,)), dma((2, phases)),
+            pltpu.VMEM((1, samples), jnp.float32),
+            pltpu.VMEM((1, comps), jnp.float32),
+            pltpu.VMEM((1, total), jnp.int32),
+            pltpu.VMEM((1, total // cpgs), jnp.int32),
+            dma((6,)), dma((AHEAD,)),
+            dma((1,)), dma((2, phases - 1, pieces)),
+            dma((1,)), dma((phases,)),
             dma((2,)), dma((2, units)),
             dma((1,)), dma((n,)),
             dma((1,)), dma((1,)),

time: 57.7 us -> 54.2 us (0.939)
  Pallas kernels: 55.5 us -> 52.1 us
    pallas_call x1, Pallas kernels: 55.5 us -> 52.1 us  [scores(): pl.pallas_call(functools.partial(score_kernel, n, cpgs), out_shape=jax.Sh...]
where the time goes in v3:
time: 54.2 us; the launch traced here: 54 us
  Pallas kernels  52.1 us (96%)
  local copies, waits for them, and re-layouts  1.26 us (2%)
  between operations  0.64 us (1%)
    pallas_call x1, Pallas kernels, scores(): pl.pallas_call(functools.partial(score_kernel, n, cpgs), out_shape=jax.Sh...  52.1 us
    squeeze x1, local copies, waits for them, and re-layouts, shards(): return (out[0, :block], out[1, :block])  1.26 us

profile of v3, /device:TPU:0, one launch (start us, length us, event | category | flops | bytes accessed | tf_op | source)
XLA Modules:
  0.0 54.0 jit_solution(7388165215602513215)
XLA Ops:
  0.6 52.1 %scores.1 = f32[8,128]{1,0:T(8,128)} custom-call(bf16[32,4096]{1,0:T(8,128)(2,1)} %w_hbm.1, bf16[32,4096]{1,0:T(8,128)(2,1)} %r_hbm.1, f32[1,4096]{1,0:T(1,128)} %bitcast.8, bf16[4096,2048]{1,0:T(8,128)(2,1)} %v_hbm.1, f32[1,2048]{1,0:T(1,128)} %bitcast.9, s32[1,256]{1,0:T(1,128)} %bitcast.10, s32[1,64]{1,0:T(1,128)} %bitcast.11), custom_call_target="tpu_custom_call" | custom-call | flops 8589934592 | bytes 16777216 | tf_op jit(solution)/shard_map/scores/pallas_call | solution.py:503
  52.7 1.3 %slice_bitcast_fusion = (f32[64]{0:T(128)}, f32[64]{0:T(128)}) fusion(f32[8,128]{1,0:T(8,128)} %scores.1), kind=kLoop, calls=%fused_computation | loop fusion | bytes 1024 | tf_op jit(solution)/shard_map/squeeze | solution.py:545

commit v4 on v3

--- a/solution.py
+++ b/solution.py
@@ -14,7 +14,7 @@
 MESH = pl.DeviceIdType.MESH
 LANES = 128
 CHUNK = 256
-SKEW = 5
+SKEW = 9
 STRIP = 512
 AHEAD = 3
 UNROLL = 4
@@ -41,6 +41,11 @@
     cols = samples // pieces
     is_end = (mz == 0) | (mz == last)
 
+    def lag_of(d, k):
+        turned = SKEW * k + (1 - d)
+        return turned // 2 if isinstance(k, int) else lax.div(turned, 2)
+
+
     def mask_of(h, j):
         return sum(bit for i, bit in enumerate(orders[h]) if (j >> i) & 1)
 
@@ -93,8 +98,6 @@
             g[0, pl.ds(h * side + half, half), at] = design[h * half : (h + 1) * half]
         return carry
 
-    with jax.named_scope("prep"):
-        lax.fori_loop(0, samples // STRIP, prepare, 0)
 
     def piece(q):
         return pl.ds(pl.multiple_of(q * cols, cols), cols)
@@ -111,9 +114,11 @@
             send_sem=ls.at[0], recv_sem=lr.at[j],
             device_id={"samp": flipped(1)}, device_id_type=MESH)
 
-    pl.semaphore_wait(barrier, n - 1 + (mz > 0).astype(jnp.int32) + (mz < last).astype(jnp.int32))
-
+    strips = cols // STRIP
     for q in range(pieces):
+        lax.fori_loop(q * strips, (q + 1) * strips, prepare, 0)
+        if q == 0:
+            pl.semaphore_wait(barrier, n - 1 + (mz > 0).astype(jnp.int32) + (mz < last).astype(jnp.int32))
         for h in range(2):
             ship(h, 0, 1, q, orders[h][0]).start()
     for q in range(pieces):
@@ -166,7 +171,7 @@
 
     def chain(d, i):
         return pltpu.make_async_remote_copy(
-            src_ref=sent.at[d, i], dst_ref=landed.at[d, i], send_sem=zs.at[d], recv_sem=zr.at[d, i],
+            src_ref=sent.at[d, i], dst_ref=landed.at[d, i], send_sem=zs.at[d], recv_sem=zr.at[d, lax.rem(i, zr.shape[1])],
             device_id={"cpg": lax.min(mz + 1, last) if d else lax.max(mz - 1, 0)}, device_id_type=MESH)
 
     def hand(d, j, c, cb):
@@ -212,12 +217,13 @@
                 def _():
                     deliver(d, i, options)
 
-    lag = SKEW * last
+    lag = max(lag_of(0, last), lag_of(1, last))
 
     def forward(t, low, high):
-        options = [j for j in range(phases) if low - lag < (j + 1) * chunks and high - lag > j * chunks]
         for d, behind in ((1, mz), (0, last - mz)):
-            i = t - SKEW * behind
+            whole = lag_of(d, last)
+            options = [j for j in range(phases) if low - whole < (j + 1) * chunks and high - whole > j * chunks]
+            i = t - lag_of(d, behind)
             with jax.named_scope("up" if d else "down"):
                 if low >= lag and high <= units:
                     advance(d, i, behind == 0, behind == last, options)
@@ -490,6 +496,8 @@
     chunks = comps // CHUNK
     phases = n // 2
     units = phases * chunks
+    furthest = max(SKEW, (SKEW * (cpgs - 1) + 1) // 2)
+    window = min(units, -(-(furthest + 1) // 8) * 8)
     half = each // 2
     pair = 2 * half
     side = 2 * pair
@@ -527,7 +535,7 @@
             dma((6,)), dma((AHEAD,)),
             dma((1,)), dma((2, phases - 1, pieces)),
             dma((1,)), dma((phases,)),
-            dma((2,)), dma((2, units)),
+            dma((2,)), dma((2, window)),
             dma((1,)), dma((n,)),
             dma((1,)), dma((1,)),
             dma((3,)), dma((3,)),

time: 54.2 us -> 53.5 us (0.987)
  Pallas kernels: 52.1 us -> 51.4 us
    pallas_call x1, Pallas kernels: 52.1 us -> 51.4 us  [scores(): pl.pallas_call(functools.partial(score_kernel, n, cpgs), out_shape=jax.Sh...]
where the time goes in v4:
time: 53.5 us; the launch traced here: 53.3 us
  Pallas kernels  51.4 us (96%)
  local copies, waits for them, and re-layouts  1.26 us (2%)
  between operations  0.64 us (1%)
    pallas_call x1, Pallas kernels, scores(): pl.pallas_call(functools.partial(score_kernel, n, cpgs), out_shape=jax.Sh...  51.4 us
    squeeze x1, local copies, waits for them, and re-layouts, shards(): return (out[0, :block], out[1, :block])  1.26 us

profile of v4, /device:TPU:0, one launch (start us, length us, event | category | flops | bytes accessed | tf_op | source)
XLA Modules:
  0.0 53.3 jit_solution(12728964585483501623)
XLA Ops:
  0.6 51.4 %scores.1 = f32[8,128]{1,0:T(8,128)} custom-call(bf16[32,4096]{1,0:T(8,128)(2,1)} %w_hbm.1, bf16[32,4096]{1,0:T(8,128)(2,1)} %r_hbm.1, f32[1,4096]{1,0:T(1,128)} %bitcast.8, bf16[4096,2048]{1,0:T(8,128)(2,1)} %v_hbm.1, f32[1,2048]{1,0:T(1,128)} %bitcast.9, s32[1,256]{1,0:T(1,128)} %bitcast.10, s32[1,64]{1,0:T(1,128)} %bitcast.11), custom_call_target="tpu_custom_call" | custom-call | flops 8589934592 | bytes 16777216 | tf_op jit(solution)/shard_map/scores/pallas_call | solution.py:511
  52.0 1.3 %slice_bitcast_fusion = (f32[64]{0:T(128)}, f32[64]{0:T(128)}) fusion(f32[8,128]{1,0:T(8,128)} %scores.1), kind=kLoop, calls=%fused_computation | loop fusion | bytes 1024 | tf_op jit(solution)/shard_map/squeeze | solution.py:553

commit v5 on v4

--- a/solution.py
+++ b/solution.py
@@ -16,8 +16,9 @@
 CHUNK = 256
 SKEW = 9
 STRIP = 512
-AHEAD = 3
-UNROLL = 4
+AHEAD = 4
+GROUP = 2
+UNROLL = 8
 
 
 def score_kernel(n, cpgs, w_hbm, r_hbm, ph_hbm, v_hbm, lam_hbm, pos_hbm, reach_hbm, out_ref,
@@ -251,7 +252,6 @@
                     load(c + AHEAD).start()
             with jax.named_scope("mm"):
                 part[t] = jnp.dot(g[j], v[c], preferred_element_type=jnp.float32)
-            forward(t, j * chunks, (j + 1) * chunks)
             nxt = j + 1
             if nxt < phases:
                 q = lax.div(c, 2)
@@ -268,6 +268,7 @@
                             turned = orders[1 - h][upper] == orders[h][top] and orders[h][upper] != orders[h][top]
                             k = 1 - h if turned else h
                             ship(k, after - (1 << upper), after, q, orders[k][upper]).start()
+            forward(t, j * chunks, (j + 1) * chunks)
             return carry
 
         lax.fori_loop(0, chunks, step, 0)
@@ -296,7 +297,8 @@
             device_id={"samp": lax.rem(me + i, n), "cpg": lax.clamp(0, home + step - 1, last)}, device_id_type=MESH)
 
     def each_post(act):
-        for step in range(3):
+        for turn_of in range(3):
+            step = jnp.where(which == 0, 2 - turn_of, turn_of)
             plane = home + step - 1
 
             @pl.when((plane >= 0) & (plane <= last))
@@ -361,7 +363,7 @@
                     return tuple(x + fold(y) for x, y in zip(acc, terms))
 
                 with jax.named_scope(f"absorb{2*j+cb}"):
-                    acc = lax.fori_loop(0, chunks, absorb, acc)
+                    acc = lax.fori_loop(0, chunks // GROUP, lambda i, acc: absorb(i * GROUP + 1, absorb(i * GROUP, acc)), acc)
         crossed, energy, s_r, s_p, s_q, traced, fisher = acc
         log_scale = newton(jnp.zeros((half, 1), jnp.float32),
                            (crossed, energy, tall(traced), tall(fisher), s_r, s_p, s_q))

time: 53.5 us -> 52.6 us (0.983)
  Pallas kernels: 51.4 us -> 50.5 us
    pallas_call x1, Pallas kernels: 51.4 us -> 50.5 us  [scores(): pl.pallas_call(functools.partial(score_kernel, n, cpgs), out_shape=jax.Sh...]
where the time goes in v5:
time: 52.6 us; the launch traced here: 52.4 us
  Pallas kernels  50.5 us (96%)
  local copies, waits for them, and re-layouts  1.26 us (2%)
  between operations  0.64 us (1%)
    pallas_call x1, Pallas kernels, scores(): pl.pallas_call(functools.partial(score_kernel, n, cpgs), out_shape=jax.Sh...  50.5 us
    squeeze x1, local copies, waits for them, and re-layouts, shards(): return (out[0, :block], out[1, :block])  1.26 us

profile of v5, /device:TPU:0, one launch (start us, length us, event | category | flops | bytes accessed | tf_op | source)
XLA Modules:
  0.0 52.4 jit_solution(5434772033870880545)
XLA Ops:
  0.6 50.5 %scores.1 = f32[8,128]{1,0:T(8,128)} custom-call(bf16[32,4096]{1,0:T(8,128)(2,1)} %w_hbm.1, bf16[32,4096]{1,0:T(8,128)(2,1)} %r_hbm.1, f32[1,4096]{1,0:T(1,128)} %bitcast.8, bf16[4096,2048]{1,0:T(8,128)(2,1)} %v_hbm.1, f32[1,2048]{1,0:T(1,128)} %bitcast.9, s32[1,256]{1,0:T(1,128)} %bitcast.10, s32[1,64]{1,0:T(1,128)} %bitcast.11), custom_call_target="tpu_custom_call" | custom-call | flops 8589934592 | bytes 16777216 | tf_op jit(solution)/shard_map/scores/pallas_call | solution.py:513
  51.1 1.3 %slice_bitcast_fusion = (f32[64]{0:T(128)}, f32[64]{0:T(128)}) fusion(f32[8,128]{1,0:T(8,128)} %scores.1), kind=kLoop, calls=%fused_computation | loop fusion | bytes 1024 | tf_op jit(solution)/shard_map/squeeze | solution.py:555
